TPU v7x, 32 devices: a whole 2x2x4 slice. The times are simulated.
32 devices in a mesh: genes: 32 (over z, y, x, core).
Axes of the slice: x: 2, y: 2, z: 4, core: 2. Of those that a mesh axis runs over, the one named last changes fastest.
Arguments:
- expression: bfloat16 [32768, 1024], P('genes'), may hold values from -10 to 20
- labels: int32 [32768], P('genes'), may hold values from 0 to 399
Outputs:
- membership: float32 [32768, 400], P('genes')
- eigengenes: bfloat16 [400, 1024], replicated
All inputs are finite; a program needn't handle non-finite values.
Results may differ from a plain program's by a relative error of at most 0.0012.
The roundings to bfloat16 on the way count: a program that leaves them out, or rounds other values in their place, can miss the bound.
Values may be sent and summed in bfloat16 or wider, within the bound.
No kernel may reach another device: no remote copies, remote signals or barrier semaphores. Data moves between devices by JAX's collectives and lax.ppermute only.
A program may use at most 64 MiB of HBM per device.

v0:
```python
import jax
import jax.numpy as jnp
from jax import lax
from jax.sharding import PartitionSpec as P

SAMPLES = 1024
MODULES = 400
ITERS = 2
epsilon = 1e-05
sharpness = 30.0


def standardize(expression):
    values = expression.astype(jnp.float32)
    centre = jnp.mean(values, axis=1, keepdims=True)
    shifted = values - centre
    spread = jnp.mean(shifted * shifted, axis=1, keepdims=True)
    return (shifted * lax.rsqrt(spread + epsilon)).astype(jnp.bfloat16)


def shards(expression, labels):
    standard = standardize(expression)
    module_ids = jnp.arange(MODULES, dtype=jnp.int32)
    weights = (labels[:, None] == module_ids[None, :]).astype(jnp.bfloat16)
    shares = None
    eigengenes = None
    for iteration in range(ITERS):
        partial_value = lax.dot_general(
            weights, standard, (((0,), (0,)), ((), ())), preferred_element_type=jnp.float32
        )
        module_sums = lax.psum(partial_value, "genes")
        scale = lax.rsqrt(jnp.mean(module_sums * module_sums, axis=1, keepdims=True) + epsilon)
        eigengenes = (module_sums * scale).astype(jnp.bfloat16)
        correlation = (
            lax.dot_general(
                standard, eigengenes, (((1,), (1,)), ((), ())), preferred_element_type=jnp.float32
            )
            / SAMPLES
        )
        raised = jnp.exp(sharpness * correlation)
        shares = raised / jnp.sum(raised, axis=1, keepdims=True)
        weights = shares.astype(jnp.bfloat16)
    return (MODULES * shares, eigengenes)


def solution(mesh):
    placed = (P("genes", None), P("genes"))
    return jax.shard_map(
        shards, mesh=mesh, in_specs=placed, out_specs=(P("genes", None), P()), check_vma=False
    )
```

profile of v0, /device:TPU:0, one launch (start us, length us, event | category | flops | bytes accessed | tf_op | source)
XLA Modules:
  0.0 299.7 jit_solution(1048506449199865023)
XLA Ops:
  7.2 0.0 copy-start
  7.2 0.0 all-reduce.3.cloned.1.call-start
  7.2 2.1 convert_reduce_fusion
  9.3 0.1 copy-done
  9.4 0.7 fusion.2
  10.1 0.0 copy-start.5
  10.1 0.5 fusion.3
  10.7 0.0 copy-start.2
  10.7 1.3 copy-done.2
  12.0 0.0 copy-done.5
  12.0 2.4 fusion.4
  14.4 0.0 copy-start.3
  14.4 0.0 all-reduce.3.cloned.1.call-update
  14.4 0.0 all-reduce.5.cloned.1.call-start
  14.5 135.1 %all-reduce.3.cloned.1.call-done = f32[400,1024]{1,0:T(8,128)} async-done(((f32[400,1024]{1,0:T(8,128)}), f32[400,1024]{1,0:T(8,128)}) %all-reduce.3.cloned.1.call-update) | async-done | bytes 1638416 | tf_op jit(solution)/shard_map/psum | solution.py:31
  149.6 1.6 multiply_reduce_fusion.1
  151.2 0.0 copy-done.3
  151.2 2.5 fusion.9
  153.7 2.2 fusion.6
  155.9 0.0 all-reduce.5.cloned.1.call-update
  155.9 132.3 %all-reduce.5.cloned.1.call-done = f32[400,1024]{1,0:T(8,128)} async-done(((f32[400,1024]{1,0:T(8,128)}), f32[400,1024]{1,0:T(8,128)}) %all-reduce.5.cloned.1.call-update) | async-done | bytes 1638416 | tf_op jit(solution)/shard_map/psum | solution.py:31
  288.3 0.0 copy-start.1
  288.3 1.7 multiply_reduce_fusion
  290.0 0.2 copy-done.1
  290.2 0.1 multiply_convert_fusion
  290.4 0.0 copy-start.4
  290.4 1.1 fusion.10
  291.5 0.0 copy-done.4
  291.5 1.4 divide_multiply_fusion
  (4 shorter events, 0.0 us)
Async XLA Ops:
  7.2 2.2 copy-start
  7.2 142.4 %all-reduce.3.cloned.1.call-start = ((), (), s32[]{:S(2)}) async-start(), calls=%async_computation | async-start | bytes 3276800 | tf_op jit(solution)/shard_map/psum | solution.py:31
  10.1 1.9 copy-start.5
  10.7 1.4 copy-start.2
  14.4 136.8 %copy-start.3 = (bf16[1024,1024]{1,0:T(8,128)(2,1)S(1)}, bf16[1024,1024]{1,0:T(8,128)(2,1)}, u32[]{:S(2)}) copy-start(bf16[1024,1024]{1,0:T(8,128)(2,1)} %copy-done.2) | copy-start | bytes 6291460
  14.4 273.8 %all-reduce.5.cloned.1.call-start = ((), (), s32[]{:S(2)}) async-start(), calls=%async_computation.1 | async-start | bytes 3276800 | tf_op jit(solution)/shard_map/psum | solution.py:31
  288.3 1.9 copy-start.1
  290.4 1.1 copy-start.4
Sparse Core Ops, SparseCore 0:
  14.6 134.9 all-reduce.2
  156.1 132.1 all-reduce.4
where the time goes:
time: 300 us
  waiting for transfers between devices  267 us (89%)
  between operations  14.1 us (5%)
  other arithmetic  8.28 us (3%)
  matrix products  8.17 us (3%)
    psum x2, waiting for transfers between devices, shards(): module_sums = lax.psum(partial_value, 'genes')  267 us
  transfers between devices with their start and end apart: 2, of which 2 were waited for; matrix products, arithmetic and copies ran while one was open for 0% of the time, Pallas kernels for 0%

commit v1 on v0

--- a/solution.py
+++ b/solution.py
@@ -28,7 +28,7 @@
         partial_value = lax.dot_general(
             weights, standard, (((0,), (0,)), ((), ())), preferred_element_type=jnp.float32
         )
-        module_sums = lax.psum(partial_value, "genes")
+        module_sums = jnp.sum(lax.all_gather(partial_value, "genes"), axis=0)
         scale = lax.rsqrt(jnp.mean(module_sums * module_sums, axis=1, keepdims=True) + epsilon)
         eigengenes = (module_sums * scale).astype(jnp.bfloat16)
         correlation = (

time: 300 us -> 635 us (2.12)
  waiting for transfers between devices: 267 us -> 571 us
  other arithmetic: 8.28 us -> 38.6 us
    all_gather x0 -> x2, waiting for transfers between devices: none -> 571 us  [shards(): module_sums = jnp.sum(lax.all_gather(partial_value, 'genes'), axis=0)]
    psum x2 -> x0, waiting for transfers between devices: 267 us -> none  [shards(): module_sums = lax.psum(partial_value, 'genes')]
    reduce_sum x0 -> x2, other arithmetic: none -> 33.3 us  [shards(): module_sums = jnp.sum(lax.all_gather(partial_value, 'genes'), axis=0)]
where the time goes in v1:
time: 635 us
  waiting for transfers between devices  571 us (90%)
  other arithmetic  38.6 us (6%)
  between operations  14.1 us (2%)
  matrix products  8.54 us (1%)
    all_gather x2, waiting for transfers between devices, shards(): module_sums = jnp.sum(lax.all_gather(partial_value, 'genes'), axis=0)  571 us
    reduce_sum x2, other arithmetic, shards(): module_sums = jnp.sum(lax.all_gather(partial_value, 'genes'), axis=0)  33.3 us
  transfers between devices with their start and end apart: 2, of which 2 were waited for; matrix products, arithmetic and copies ran while one was open for 0% of the time, Pallas kernels for 0%

profile of v1, /device:TPU:0, one launch (start us, length us, event | category | flops | bytes accessed | tf_op | source)
XLA Modules:
  0.0 635.0 jit_solution(12211244244536334628)
XLA Ops:
  7.2 0.0 copy-start
  7.2 0.0 all-gather.5.cloned.1.call-start
  7.2 2.1 convert_reduce_fusion
  9.3 0.1 copy-done
  9.4 0.7 fusion.2
  10.1 0.0 copy-start.5
  10.1 0.5 fusion.3
  10.7 0.0 copy-start.1
  10.7 1.4 copy-done.1
  12.0 0.0 copy-done.5
  12.0 2.4 fusion.4
  14.4 0.0 all-gather.5.cloned.1.call-update
  14.4 0.0 all-gather.7.cloned.1.call-start
  14.5 287.6 %all-gather.5.cloned.1.call-done = f32[12800,1024]{1,0:T(8,128)} async-done(((f32[400,1024]{1,0:T(8,128)}), f32[12800,1024]{1,0:T(8,128)}) %all-gather.5.cloned.1.call-update) | async-done | bytes 52428816 | tf_op jit(solution)/shard_map/all_gather | solution.py:31
  302.1 16.7 %reduce_sum.74 = f32[400,1024]{1,0:T(8,128)S(1)} reduce(f32[32,400,1024]{2,1,0:T(8,128)} %bitcast.7, f32[]{:T(128)} %constant.16.clone.1), dimensions={0}, to_apply=%region_2.0 | reduce | flops 12697600 | bytes 54067204 | tf_op jit(solution)/shard_map/reduce_sum | solution.py:31
  318.8 0.2 multiply_reduce_fusion.1
  319.0 0.0 copy-start.2
  319.0 2.8 fusion.9
  321.8 0.0 copy-done.2
  321.8 2.2 fusion.6
  324.0 0.0 all-gather.7.cloned.1.call-update
  324.1 283.1 %all-gather.7.cloned.1.call-done = f32[12800,1024]{1,0:T(8,128)} async-done(((f32[400,1024]{1,0:T(8,128)}), f32[12800,1024]{1,0:T(8,128)}) %all-gather.7.cloned.1.call-update) | async-done | bytes 52428816 | tf_op jit(solution)/shard_map/all_gather | solution.py:31
  607.2 16.7 %reduce_sum.77 = f32[400,1024]{1,0:T(8,128)S(1)} reduce(f32[32,400,1024]{2,1,0:T(8,128)} %bitcast.8, f32[]{:T(128)} %constant.16.clone.1), dimensions={0}, to_apply=%region_5.0 | reduce | flops 12697600 | bytes 54067204 | tf_op jit(solution)/shard_map/reduce_sum | solution.py:31
  623.8 0.2 multiply_reduce_fusion
  624.0 0.0 copy-start.3
  624.0 0.2 multiply_convert_fusion
  624.2 1.4 copy-done.3
  625.6 0.0 copy-start.4
  625.6 1.1 fusion.10
  626.7 0.0 copy-done.4
  626.7 1.4 divide_multiply_fusion
  (4 shorter events, 0.0 us)
Async XLA Ops:
  7.2 2.2 copy-start
  7.2 294.9 %all-gather.5.cloned.1.call-start = ((), (), s32[]{:S(2)}) async-start(), calls=%async_computation | async-start | bytes 54067200 | tf_op jit(solution)/shard_map/all_gather | solution.py:31
  10.1 1.9 copy-start.5
  10.7 1.4 copy-start.1
  14.4 592.7 %all-gather.7.cloned.1.call-start = ((), (), s32[]{:S(2)}) async-start(), calls=%async_computation.1 | async-start | bytes 54067200 | tf_op jit(solution)/shard_map/all_gather | solution.py:31
  319.0 2.8 copy-start.2
  624.0 1.6 copy-start.3
  625.6 1.1 copy-start.4
Sparse Core Ops, SparseCore 0:
  14.6 287.4 all-gather.4
  324.2 282.9 all-gather.6
